TPU v7x, 32 devices: a whole 2x2x4 slice. The times are simulated.
32 devices in a mesh: dp: 4 (over z), stage: 2 (over y), tp: 4 (over x, core).
Axes of the slice: x: 2, y: 2, z: 4, core: 2. Of those that a mesh axis runs over, the one named last changes fastest.
Arguments:
- act_in: bfloat16 [2, 64, 14, 14, 512], P('stage', ('dp', 'tp'))
- conv_w: bfloat16 [2, 3, 3, 512, 1024], P('stage', None, None, 'tp')
- scale_vec: float32 [2, 1024], P('stage', 'tp')
- shift_vec: float32 [2, 1024], P('stage', 'tp')
- grad_z: bfloat16 [2, 64, 14, 14, 1024], P('stage', 'dp', None, None, 'tp')
Outputs:
- output 1: bfloat16 [2, 64, 14, 14, 1024], P('stage', 'dp', None, None, 'tp')
- output 2: bfloat16 [2, 64, 14, 14, 512], P('stage', ('dp', 'tp'))
- output 3: float32 [2, 3, 3, 512, 1024], P('stage', None, None, 'tp')
All inputs are finite; a program needn't handle non-finite values.
Results may differ from a plain program's by a relative error of at most 0.00771.
Values are sent between devices in bfloat16 or wider.
A program may use at most 1 GiB of HBM per device.

v0:
```python
import jax
import jax.numpy as jnp
from jax import lax
from jax.sharding import PartitionSpec as P


def conv_forward(images, kernel):
    return lax.conv_general_dilated(images, kernel, (1, 1), "SAME", dimension_numbers=("NHWC", "HWIO", "NHWC"), preferred_element_type=jnp.float32)


def conv_input_grad(grad_out, kernel):
    return lax.conv_general_dilated(grad_out, kernel[::-1, ::-1], (1, 1), "SAME", dimension_numbers=("NHWC", "HWOI", "NHWC"), preferred_element_type=jnp.float32)


def conv_kernel_grad(images, grad_out):
    return lax.conv_general_dilated(images, grad_out, (1, 1), ((1, 1), (1, 1)), dimension_numbers=("CHWN", "IHWO", "HWNC"), preferred_element_type=jnp.float32)


def solution(mesh):
    def body(act_loc, w_loc, scale_loc, shift_loc, grad_loc):
        images = act_loc[0]
        moved = lax.all_to_all(images, "tp", 3, 0, tiled=True)
        act_blk = lax.ppermute(moved, "stage", perm=[(0, 1)])
        kernel = w_loc[0]
        part_sum = conv_forward(act_blk, kernel)
        pre_out = lax.psum_scatter(part_sum, "tp", scatter_dimension=3, tiled=True)
        lin_out = pre_out * scale_loc[0] + shift_loc[0]
        z_blk = jnp.maximum(lin_out, 0.0).astype(jnp.bfloat16)
        grad_blk = jnp.where(lin_out > 0, grad_loc[0].astype(jnp.float32) * scale_loc[0], 0.0).astype(jnp.bfloat16)
        grad_full = lax.all_gather(grad_blk, "tp", axis=3, tiled=True)
        dact_blk = conv_input_grad(grad_full, kernel).astype(jnp.bfloat16)
        dw_part = conv_kernel_grad(act_blk, grad_full)
        dw_blk = lax.psum(dw_part, "dp")
        dact_back = lax.ppermute(dact_blk, "stage", perm=[(1, 0)])
        dact_img = lax.all_to_all(dact_back, "tp", 0, 3, tiled=True)
        return z_blk[None], dact_img[None], dw_blk[None]

    act_spec = P("stage", ("dp", "tp"))
    w_spec = P("stage", None, None, "tp")
    vec_spec = P("stage", "tp")
    grad_spec = P("stage", "dp", None, None, "tp")
    return jax.shard_map(body, mesh=mesh, in_specs=(act_spec, w_spec, vec_spec, vec_spec, grad_spec), out_specs=(grad_spec, act_spec, w_spec), check_vma=False)
```

profile of v0, /device:TPU:0, one launch (start us, length us, event | category | flops | bytes accessed | tf_op | source)
XLA Modules:
  0.0 468.4 jit_solution(15502937029799498214)
XLA Ops:
  7.2 0.0 copy-start
  7.2 0.0 reduce-scatter.2.cloned.1.call-start
  7.2 9.8 %copy.14 = bf16[1,4,14,14,512]{3,1,2,4,0:T(4,128)(2,1)} copy(bf16[1,4,14,14,512]{4,1,3,2,0:T(4,128)(2,1)} %param.5) | data formatting | bytes 1605632 | tf_op args[0]
  17.0 8.5 %bitcast_bitcast_fusion = bf16[512,14,4,14]{3,2,1,0:T(4,128)(2,1)} fusion(bf16[1,4,14,14,512]{3,1,2,4,0:T(4,128)(2,1)} %copy.14), kind=kLoop, calls=%fused_computation.12 | loop fusion | bytes 1605632
  25.6 15.1 %reshape.12 = bf16[4,2,50176]{2,1,0:T(2,128)(2,1)S(1)} reshape(bf16[512,14,4,14]{3,2,1,0:T(4,128)(2,1)} %bitcast_bitcast_fusion) | data formatting | bytes 1605632
  40.6 15.9 %all_to_all.33 = bf16[4,2,50176]{2,1,0:T(2,128)(2,1)} all-to-all(bf16[4,2,50176]{2,1,0:T(2,128)(2,1)S(1)} %reshape.12), channel_id=1, replica_groups=mesh['dp'=4,'stage'=2,'tp'=4] {'tp'}, dimensions={0} | all-to-all | bytes 1605632 | tf_op jit(solution)/shard_map/all_to_all | solution.py:22
  56.5 20.5 %reshape.13 = bf16[512,14,4,14]{3,2,1,0:T(4,128)(2,1)} reshape(bf16[4,2,50176]{2,1,0:T(2,128)(2,1)} %all_to_all.33) | data formatting | bytes 1605632
  77.0 10.9 %copy.15 = bf16[4,14,14,4,128]{4,0,3,2,1:T(4,128)(2,1)S(1)} copy(bf16[4,14,14,4,128]{2,0,1,4,3:T(4,128)(2,1)} %bitcast.34) | data formatting | bytes 1605632 | tf_op jit(solution)/shard_map/all_to_all | solution.py:22
  88.0 4.1 collective-permute-start
  92.1 17.2 %collective-permute-done = bf16[16,14,14,128]{3,0,2,1:T(8,128)(2,1)S(1)} collective-permute-done((bf16[16,14,14,128]{3,0,2,1:T(8,128)(2,1)S(1)}, bf16[16,14,14,128]{3,0,2,1:T(8,128)(2,1)S(1)}, u32[]{:S(2)}, u32[]{:S(2)}) %collective-permute-start) | collective-permute-done | bytes 802848 | tf_op jit(solution)/shard_map/ppermute | solution.py:23
  109.3 0.9 copy-done.3
  110.1 0.0 copy-done
  110.1 11.4 %fusion.4 = f32[16,14,14,1024]{3,0,2,1:T(8,128)} fusion(bf16[16,14,14,128]{3,0,2,1:T(8,128)(2,1)S(1)} %collective-permute-done, bf16[1,3,3,128,1024]{4,3,2,1,0:T(8,128)(2,1)S(1)} %copy-done), kind=kOutput, calls=%fused_computation.7 | convolution fusion | flops 6710886400 | bytes 16007168 | tf_op jit(solution)/shard_map/conv_general_dilated | solution.py:8
  121.5 0.0 reduce-scatter.2.cloned.1.call-update
  121.6 0.0 all-gather.2.cloned.1.call-start
  121.6 99.1 %reduce-scatter.2.cloned.1.call-done = f32[16,14,14,256]{3,0,2,1:T(8,128)} async-done(((f32[16,14,14,1024]{3,0,2,1:T(8,128)}), f32[16,14,14,256]{3,0,2,1:T(8,128)}) %reduce-scatter.2.cloned.1.call-update) | async-done | bytes 3211280 | tf_op jit(solution)/shard_map/reduce_scatter | solution.py:26
  220.7 0.0 copy-done.1
  220.7 5.0 %fusion.1 = (bf16[16,14,14,256]{3,0,2,1:T(8,128)(2,1)}, bf16[1,16,14,14,256]{4,1,3,2,0:T(8,128)(2,1)}) fusion(f32[16,14,14,256]{3,0,2,1:T(8,128)} %reduce-scatter.2.cloned.1.call-done, bf16[1,16,14,14,256]{4,1,3,2,0:T(8,128)(2,1)} %param.9, f32[256]{0:T(256)S(1)} %bitcast.37, f32[256]{0:T(256)S(1)} %bitcast.38), kind=kLoop, calls=%fused_computation.2 | loop fusion | flops 7225344 | bytes 8030208 | tf_op jit(solution)/shard_map/convert_element_type | solution.py:29
  225.8 0.0 all-gather.2.cloned.1.call-update
  225.8 0.0 all-reduce.2.cloned.1.call-start
  225.8 48.1 %all-gather.2.cloned.1.call-done = bf16[16,14,14,1024]{3,0,2,1:T(8,128)(2,1)} async-done(((bf16[16,14,14,256]{3,0,2,1:T(8,128)(2,1)}), bf16[16,14,14,1024]{3,0,2,1:T(8,128)(2,1)}) %all-gather.2.cloned.1.call-update) | async-done | bytes 6422544 | tf_op jit(solution)/shard_map/all_gather | solution.py:30
  273.9 11.7 %convolution_bitcast_fusion = f32[1,3,3,128,1024]{4,3,2,1,0:T(8,128)} fusion(bf16[16,14,14,128]{3,0,2,1:T(8,128)(2,1)S(1)} %copy-done.4, bf16[16,14,14,1024]{3,0,2,1:T(8,128)(2,1)} %all-gather.2.cloned.1.call-done), kind=kOutput, calls=%fused_computation.9 | convolution fusion | flops 6710886400 | bytes 11943936 | tf_op jit(solution)/shard_map/conv_general_dilated | solution.py:16
  285.6 0.0 all-reduce.2.cloned.1.call-update
  285.6 17.3 %fusion.7 = bf16[16,14,14,128]{3,0,2,1:T(8,128)(2,1)S(1)} fusion(bf16[16,14,14,1024]{3,0,2,1:T(8,128)(2,1)} %all-gather.2.cloned.1.call-done, bf16[1,3,3,128,1024]{4,3,2,1,0:T(8,128)(2,1)S(1)} %copy-done), kind=kOutput, calls=%fused_computation.11 | convolution fusion | flops 6711287808 | bytes 9584640 | tf_op jit(solution)/shard_map/conv_general_dilated | solution.py:12
  303.0 1.3 collective-permute-start.1
  304.3 20.6 %collective-permute-done.1 = bf16[16,14,14,128]{3,0,2,1:T(8,128)(2,1)S(1)} collective-permute-done((bf16[16,14,14,128]{3,0,2,1:T(8,128)(2,1)S(1)}, bf16[16,14,14,128]{3,0,2,1:T(8,128)(2,1)S(1)}, u32[]{:S(2)}, u32[]{:S(2)}) %collective-permute-start.1) | collective-permute-done | bytes 802848 | tf_op jit(solution)/shard_map/ppermute | solution.py:34
  324.9 0.2 copy.16
  325.1 15.4 %all_to_all.34 = bf16[16,14,14,128]{3,2,1,0:T(8,128)(2,1)S(1)} all-to-all(bf16[16,14,14,128]{3,2,1,0:T(8,128)(2,1)S(1)} %copy.16), channel_id=1, replica_groups=mesh['dp'=4,'stage'=2,'tp'=4] {'tp'}, dimensions={0} | all-to-all | bytes 1605632 | tf_op jit(solution)/shard_map/all_to_all | solution.py:35
  340.6 0.6 copy.17
  341.2 1.2 broadcast_in_dim.12
  342.4 114.2 %all-reduce.2.cloned.1.call-done = f32[1,3,3,128,1024]{4,3,2,1,0:T(8,128)} async-done(((f32[1,3,3,128,1024]{4,3,2,1,0:T(8,128)}), f32[1,3,3,128,1024]{4,3,2,1,0:T(8,128)}) %all-reduce.2.cloned.1.call-update) | async-done | bytes 4718608 | tf_op jit(solution)/shard_map/psum | solution.py:33
  456.6 5.2 %copy.19 = f32[1,3,3,128,1024]{4,3,2,1,0:T(8,128)} copy(f32[1,3,3,128,1024]{4,3,2,1,0:T(8,128)} %all-reduce.2.cloned.1.call-done) | data formatting | bytes 9437184
  (6 shorter events, 0.0 us)
Async XLA Ops:
  7.2 103.0 %copy-start = (bf16[1,3,3,128,1024]{4,3,2,1,0:T(8,128)(2,1)S(1)}, bf16[1,3,3,128,1024]{4,3,2,1,0:T(8,128)(2,1)}, u32[]{:S(2)}) copy-start(bf16[1,3,3,128,1024]{4,3,2,1,0:T(8,128)(2,1)} %param.6) | copy-start | bytes 7077892
  7.2 213.5 %reduce-scatter.2.cloned.1.call-start = ((), (), s32[]{:S(2)}) async-start(), calls=%async_computation.3 | async-start | bytes 16056320 | tf_op jit(solution)/shard_map/reduce_scatter | solution.py:26
  88.0 21.3 %collective-permute-start = (bf16[16,14,14,128]{3,0,2,1:T(8,128)(2,1)S(1)}, bf16[16,14,14,128]{3,0,2,1:T(8,128)(2,1)S(1)}, u32[]{:S(2)}, u32[]{:S(2)}) collective-permute-start(bf16[16,14,14,128]{3,0,2,1:T(8,128)(2,1)S(1)} %bitcast.36), channel_id=1, source_target_pairs={{0,4},{1,5},{2,6},{3,7},{8,12},{9,13},{10,14},{11,15},{16,20},{17,... | collective-permute-start | bytes 2408456 | tf_op jit(solution)/shard_map/ppermute | solution.py:23
  109.3 0.9 copy-start.3
  121.5 99.2 %copy-start.1 = (f32[1,256]{1,0:T(1,128)S(1)}, f32[1,256]{1,0:T(1,128)}, u32[]{:S(2)}) copy-start(f32[1,256]{1,0:T(1,128)} %param.8) | copy-start | bytes 3076
  121.5 99.2 %copy-start.2 = (f32[1,256]{1,0:T(1,128)S(1)}, f32[1,256]{1,0:T(1,128)}, u32[]{:S(2)}) copy-start(f32[1,256]{1,0:T(1,128)} %param.7) | copy-start | bytes 3076
  121.6 152.4 %all-gather.2.cloned.1.call-start = ((), (), s32[]{:S(2)}) async-start(), calls=%async_computation.4 | async-start | bytes 8028160 | tf_op jit(solution)/shard_map/all_gather | solution.py:30
  220.7 53.2 %copy-start.4 = (bf16[16,14,14,128]{3,0,2,1:T(8,128)(2,1)S(1)}, bf16[16,14,14,128]{3,0,2,1:T(8,128)(2,1)}, u32[]{:S(2)}) copy-start(bf16[16,14,14,128]{3,0,2,1:T(8,128)(2,1)} %copy-done.3) | copy-start | bytes 2408452
  225.8 230.8 %all-reduce.2.cloned.1.call-start = ((), (), s32[]{:S(2)}) async-start(), calls=%async_computation.5 | async-start | bytes 9437184 | tf_op jit(solution)/shard_map/psum | solution.py:33
  303.0 21.9 %collective-permute-start.1 = (bf16[16,14,14,128]{3,0,2,1:T(8,128)(2,1)S(1)}, bf16[16,14,14,128]{3,0,2,1:T(8,128)(2,1)S(1)}, u32[]{:S(2)}, u32[]{:S(2)}) collective-permute-start(bf16[16,14,14,128]{3,0,2,1:T(8,128)(2,1)S(1)} %fusion.7), channel_id=1, source_target_pairs={{4,0},{5,1},{6,2},{7,3},{12,8},{13,9},{14,10},{15,11},{20,16},{21,... | collective-permute-start | bytes 2408456 | tf_op jit(solution)/shard_map/ppermute | solution.py:34
Sparse Core Ops, SparseCore 0:
  121.7 98.9 reduce-scatter.1
  225.9 47.9 all-gather.1
  285.7 170.8 all-reduce.1
where the time goes:
time: 469 us; the launch traced here: 468 us
  waiting for transfers between devices  299 us (64%)
  local copies, waits for them, and re-layouts  73 us (16%)
  matrix products  40.4 us (9%)
  blocking collectives  31.3 us (7%)
  between operations  13.8 us (3%)
  starting transfers between devices  5.53 us (1%)
  other arithmetic  5.04 us (1%)
    psum x1, waiting for transfers between devices, body(): dw_blk = lax.psum(dw_part, 'dp')  114 us
    reduce_scatter x1, waiting for transfers between devices, body(): pre_out = lax.psum_scatter(part_sum, 'tp', scatter_dimension=3, tiled=True)  99.1 us
    unnamed x15, local copies, waits for them, and re-layouts  60.1 us
    all_gather x1, waiting for transfers between devices, body(): grad_full = lax.all_gather(grad_blk, 'tp', axis=3, tiled=True)  48.1 us
    ppermute x1, waiting for transfers between devices, body(): dact_back = lax.ppermute(dact_blk, 'stage', perm=[(1, 0)])  20.6 us
    conv_general_dilated x1, matrix products, conv_input_grad(): lax.conv_general_dilated(grad_out, kernel[::-1, ::-1], (1, 1), 'SAME', di...  17.3 us
    ppermute x1, waiting for transfers between devices, body(): act_blk = lax.ppermute(moved, 'stage', perm=[(0, 1)])  17.2 us
    all_to_all x1, blocking collectives, body(): moved = lax.all_to_all(images, 'tp', 3, 0, tiled=True)  15.9 us
  transfers between devices with their start and end apart: 5, of which 5 were waited for; matrix products, arithmetic and copies ran while one was open for 4% of the time, Pallas kernels for 0%

commit v1 on v0

--- a/solution.py
+++ b/solution.py
@@ -18,19 +18,21 @@
 
 def solution(mesh):
     def body(act_loc, w_loc, scale_loc, shift_loc, grad_loc):
-        images = act_loc[0]
-        moved = lax.all_to_all(images, "tp", 3, 0, tiled=True)
-        act_blk = lax.ppermute(moved, "stage", perm=[(0, 1)])
+        t = lax.axis_index("tp")
         kernel = w_loc[0]
-        part_sum = conv_forward(act_blk, kernel)
-        pre_out = lax.psum_scatter(part_sum, "tp", scatter_dimension=3, tiled=True)
+        moved = lax.ppermute(act_loc[0], "stage", perm=[(0, 1)])
+        kernel_co = lax.all_to_all(kernel, "tp", 3, 2, tiled=True)
+        act_all = lax.all_gather(moved, "tp", axis=0, tiled=True)
+        pre_out = conv_forward(act_all, kernel_co)
         lin_out = pre_out * scale_loc[0] + shift_loc[0]
         z_blk = jnp.maximum(lin_out, 0.0).astype(jnp.bfloat16)
         grad_blk = jnp.where(lin_out > 0, grad_loc[0].astype(jnp.float32) * scale_loc[0], 0.0).astype(jnp.bfloat16)
         grad_full = lax.all_gather(grad_blk, "tp", axis=3, tiled=True)
-        dact_blk = conv_input_grad(grad_full, kernel).astype(jnp.bfloat16)
+        cc = kernel.shape[2]
+        act_blk = lax.dynamic_slice_in_dim(act_all, t * cc, cc, axis=3)
         dw_part = conv_kernel_grad(act_blk, grad_full)
         dw_blk = lax.psum(dw_part, "dp")
+        dact_blk = conv_input_grad(grad_full, kernel).astype(jnp.bfloat16)
         dact_back = lax.ppermute(dact_blk, "stage", perm=[(1, 0)])
         dact_img = lax.all_to_all(dact_back, "tp", 0, 3, tiled=True)
         return z_blk[None], dact_img[None], dw_blk[None]

time: 469 us -> 360 us (0.77)
  waiting for transfers between devices: 299 us -> 201 us
  local copies, waits for them, and re-layouts: 73 us -> 23.2 us
  blocking collectives: 31.3 us -> 75.2 us
  other arithmetic: 5.04 us -> 0 us
    reduce_scatter x1 -> x0, waiting for transfers between devices: 99.1 us -> none  [body(): pre_out = lax.psum_scatter(part_sum, 'tp', scatter_dimension=3, tiled=True)]
    unnamed x15 -> x12, local copies, waits for them, and re-layouts: 60.1 us -> 10.1 us
    all_to_all x1, blocking collectives: 15.9 us -> 59.8 us  [body(): kernel_co = lax.all_to_all(kernel, 'tp', 3, 2, tiled=True)]
    all_to_all x1, local copies, waits for them, and re-layouts: 10.9 us -> 5.61 us  [body(): kernel_co = lax.all_to_all(kernel, 'tp', 3, 2, tiled=True)]
    convert_element_type x1 -> x0, other arithmetic: 5.04 us -> none  [body(): jnp.where(lin_out > 0, grad_loc[0].astype(jnp.float32) * scale_loc[0], 0.0)]
  transfers between devices with their start and end apart: 5 -> 5, of which waited for: 5 -> 4; matrix products, arithmetic and copies ran while one was open for 4% -> 8% of each run, Pallas kernels for 0% -> 0%
where the time goes in v1:
time: 360 us; the launch traced here: 359 us
  waiting for transfers between devices  201 us (56%)
  blocking collectives  75.2 us (21%)
  matrix products  39.3 us (11%)
  local copies, waits for them, and re-layouts  23.2 us (6%)
  between operations  13.9 us (4%)
  starting transfers between devices  6.58 us (2%)
    psum x1, waiting for transfers between devices, body(): dw_blk = lax.psum(dw_part, 'dp')  114 us
    all_to_all x1, blocking collectives, body(): kernel_co = lax.all_to_all(kernel, 'tp', 3, 2, tiled=True)  59.8 us
    all_gather x1, waiting for transfers between devices, body(): grad_full = lax.all_gather(grad_blk, 'tp', axis=3, tiled=True)  49.1 us
    ppermute x1, waiting for transfers between devices, body(): dact_back = lax.ppermute(dact_blk, 'stage', perm=[(1, 0)])  20.6 us
    conv_general_dilated x1, matrix products, conv_input_grad(): lax.conv_general_dilated(grad_out, kernel[::-1, ::-1], (1, 1), 'SAME', di...  17.3 us
    ppermute x1, waiting for transfers between devices, body(): moved = lax.ppermute(act_loc[0], 'stage', perm=[(0, 1)])  17.1 us
    all_to_all x1, blocking collectives, body(): dact_img = lax.all_to_all(dact_back, 'tp', 0, 3, tiled=True)  15.4 us
    conv_general_dilated x1, matrix products, conv_kernel_grad(): lax.conv_general_dilated(images, grad_out, (1, 1), ((1, 1), (1, 1)), dime...  11.9 us
  transfers between devices with their start and end apart: 5, of which 4 were waited for; matrix products, arithmetic and copies ran while one was open for 8% of the time, Pallas kernels for 0%

profile of v1, /device:TPU:0, one launch (start us, length us, event | category | flops | bytes accessed | tf_op | source)
XLA Modules:
  0.0 359.2 jit_solution(2070553375175598467)
XLA Ops:
  7.2 0.0 all-gather.3.cloned.1.call-start
  7.2 5.0 %collective-permute-start = (bf16[4,14,14,512]{3,0,2,1:T(4,128)(2,1)}, bf16[4,14,14,512]{3,0,2,1:T(4,128)(2,1)S(1)}, u32[]{:S(2)}, u32[]{:S(2)}) collective-permute-start(bf16[4,14,14,512]{3,0,2,1:T(4,128)(2,1)} %bitcast.29), channel_id=1, source_target_pairs={{0,4},{1,5},{2,6},{3,7},{8,12},{9,13},{10,14},{11,15},{16,20},{17,... | collective-permute-start | bytes 2408456 | tf_op jit(solution)/shard_map/ppermute | solution.py:23
  12.2 17.1 %collective-permute-done = bf16[4,14,14,512]{3,0,2,1:T(4,128)(2,1)S(1)} collective-permute-done((bf16[4,14,14,512]{3,0,2,1:T(4,128)(2,1)}, bf16[4,14,14,512]{3,0,2,1:T(4,128)(2,1)S(1)}, u32[]{:S(2)}, u32[]{:S(2)}) %collective-permute-start) | collective-permute-done | bytes 802848 | tf_op jit(solution)/shard_map/ppermute | solution.py:23
  29.3 1.1 copy.18
  30.4 0.0 all-gather.3.cloned.1.call-update
  30.4 0.0 all-gather.5.cloned.1.call-start
  30.5 4.8 %copy.19 = bf16[1,3,3,128,1024]{3,2,1,4,0:T(4,128)(2,1)S(1)} copy(bf16[1,3,3,128,1024]{4,3,2,1,0:T(8,128)(2,1)} %param.6) | data formatting | bytes 4718592 | tf_op args[1]
  35.3 59.8 %all_to_all.33 = bf16[3,3,128,1024]{2,1,0,3:T(4,128)(2,1)} all-to-all(bf16[3,3,128,1024]{2,1,0,3:T(4,128)(2,1)S(1)} %bitcast.24), channel_id=1, replica_groups=mesh['dp'=4,'stage'=2,'tp'=4] {'tp'}, dimensions={3} | all-to-all | bytes 4718592 | tf_op jit(solution)/shard_map/all_to_all | solution.py:24
  95.1 5.6 %copy.20 = bf16[3,3,128,4,256]{4,2,3,1,0:T(8,128)(2,1)} copy(bf16[3,3,128,4,256]{2,1,0,4,3:T(4,128)(2,1)} %bitcast.26) | data formatting | bytes 4718592 | tf_op jit(solution)/shard_map/all_to_all | solution.py:24
  100.7 0.0 copy-start.2
  100.7 4.3 %copy.21 = bf16[16,14,14,512]{3,0,2,1:T(8,128)(2,1)S(1)} copy(bf16[16,14,14,512]{3,2,1,0:T(8,128)(2,1)} %all-gather.3.cloned.1.call-done) | data formatting | bytes 6422528 | tf_op jit(solution)/shard_map/all_gather | solution.py:25
  105.0 0.0 copy-start
  105.0 0.0 copy-done.3
  105.1 0.0 copy-done.4
  105.1 0.0 copy-done.1
  105.1 0.0 copy-done.2
  105.1 10.0 %fusion.1 = (bf16[16,14,14,256]{3,0,2,1:T(8,128)(2,1)}, bf16[1,16,14,14,256]{4,1,3,2,0:T(8,128)(2,1)}) fusion(bf16[1,16,14,14,256]{4,1,3,2,0:T(8,128)(2,1)S(1)} %copy-done.2, f32[256]{0:T(256)S(1)} %bitcast.30, f32[256]{0:T(256)S(1)} %bitcast.31, bf16[16,14,14,512]{3,0,2,1:T(8,128)(2,1)S(1)} %copy.21, bf16[3,3,512,256]{3,2,1,0:T(8,128)(2,1)S(1)} %bitcast.28), kind=kOutput, calls=%fused_computation.2 | convolution fusion | flops 6718111744 | bytes 10389504 | tf_op jit(solution)/shard_map/conv_general_dilated | solution.py:8
  115.1 0.0 copy-done
  115.1 0.0 all-gather.5.cloned.1.call-update
  115.2 0.2 all-reduce.2.cloned.1.call-start
  115.4 49.1 %all-gather.5.cloned.1.call-done = bf16[16,14,14,1024]{3,0,2,1:T(8,128)(2,1)} async-done(((bf16[16,14,14,256]{3,0,2,1:T(8,128)(2,1)}), bf16[16,14,14,1024]{3,0,2,1:T(8,128)(2,1)}) %all-gather.5.cloned.1.call-update) | async-done | bytes 6422544 | tf_op jit(solution)/shard_map/all_gather | solution.py:30
  164.5 11.9 %convolution_bitcast_fusion = f32[1,3,3,128,1024]{4,3,2,1,0:T(8,128)} fusion(bf16[16,14,14,1024]{3,0,2,1:T(8,128)(2,1)} %all-gather.5.cloned.1.call-done, bf16[16,14,14,512]{3,0,2,1:T(8,128)(2,1)} %copy-done, s32[]{:T(128)S(6)} %select_n.8), kind=kOutput, calls=%fused_computation.7 | convolution fusion | flops 6710886400 | bytes 11943940 | tf_op jit(solution)/shard_map/conv_general_dilated | solution.py:16
  176.4 0.0 all-reduce.2.cloned.1.call-update
  176.5 17.3 %fusion.5 = bf16[16,14,14,128]{3,0,2,1:T(8,128)(2,1)S(1)} fusion(bf16[16,14,14,1024]{3,0,2,1:T(8,128)(2,1)} %all-gather.5.cloned.1.call-done, bf16[3,3,128,1024]{2,1,0,3:T(4,128)(2,1)S(1)} %bitcast.25), kind=kOutput, calls=%fused_computation.9 | convolution fusion | flops 6711287808 | bytes 9584640 | tf_op jit(solution)/shard_map/conv_general_dilated | solution.py:12
  193.8 1.3 collective-permute-start.1
  195.1 20.6 %collective-permute-done.1 = bf16[16,14,14,128]{3,0,2,1:T(8,128)(2,1)S(1)} collective-permute-done((bf16[16,14,14,128]{3,0,2,1:T(8,128)(2,1)S(1)}, bf16[16,14,14,128]{3,0,2,1:T(8,128)(2,1)S(1)}, u32[]{:S(2)}, u32[]{:S(2)}) %collective-permute-start.1) | collective-permute-done | bytes 802848 | tf_op jit(solution)/shard_map/ppermute | solution.py:36
  215.7 0.2 copy.23
  216.0 15.4 %all_to_all.34 = bf16[16,14,14,128]{3,2,1,0:T(8,128)(2,1)S(1)} all-to-all(bf16[16,14,14,128]{3,2,1,0:T(8,128)(2,1)S(1)} %copy.23), channel_id=1, replica_groups=mesh['dp'=4,'stage'=2,'tp'=4] {'tp'}, dimensions={0} | all-to-all | bytes 1605632 | tf_op jit(solution)/shard_map/all_to_all | solution.py:37
  231.4 0.6 copy.24
  232.0 1.2 broadcast_in_dim.12
  233.2 114.2 %all-reduce.2.cloned.1.call-done = f32[1,3,3,128,1024]{4,3,2,1,0:T(8,128)} async-done(((f32[1,3,3,128,1024]{4,3,2,1,0:T(8,128)}), f32[1,3,3,128,1024]{4,3,2,1,0:T(8,128)}) %all-reduce.2.cloned.1.call-update) | async-done | bytes 4718608 | tf_op jit(solution)/shard_map/psum | solution.py:34
  347.4 5.2 %copy.31 = f32[1,3,3,128,1024]{4,3,2,1,0:T(8,128)} copy(f32[1,3,3,128,1024]{4,3,2,1,0:T(8,128)} %all-reduce.2.cloned.1.call-done) | data formatting | bytes 9437184
  (4 shorter events, 0.0 us)
Async XLA Ops:
  7.2 93.5 %all-gather.3.cloned.1.call-start = ((), (), s32[]{:S(2)}) async-start(), calls=%async_computation.2 | async-start | bytes 4587520 | tf_op jit(solution)/shard_map/all_gather | solution.py:25
  7.2 22.1 %collective-permute-start = (bf16[4,14,14,512]{3,0,2,1:T(4,128)(2,1)}, bf16[4,14,14,512]{3,0,2,1:T(4,128)(2,1)S(1)}, u32[]{:S(2)}, u32[]{:S(2)}) collective-permute-start(bf16[4,14,14,512]{3,0,2,1:T(4,128)(2,1)} %bitcast.29), channel_id=1, source_target_pairs={{0,4},{1,5},{2,6},{3,7},{8,12},{9,13},{10,14},{11,15},{16,20},{17,... | collective-permute-start | bytes 2408456 | tf_op jit(solution)/shard_map/ppermute | solution.py:23
  30.4 134.1 %all-gather.5.cloned.1.call-start = ((), (), s32[]{:S(2)}) async-start(), calls=%async_computation.3 | async-start | bytes 8028160 | tf_op jit(solution)/shard_map/all_gather | solution.py:30
  100.7 4.4 %copy-start.3 = (f32[1,256]{1,0:T(1,128)S(1)}, f32[1,256]{1,0:T(1,128)}, u32[]{:S(2)}) copy-start(f32[1,256]{1,0:T(1,128)} %param.8) | copy-start | bytes 3076
  100.7 4.4 %copy-start.4 = (f32[1,256]{1,0:T(1,128)S(1)}, f32[1,256]{1,0:T(1,128)}, u32[]{:S(2)}) copy-start(f32[1,256]{1,0:T(1,128)} %param.7) | copy-start | bytes 3076
  100.7 4.4 %copy-start.1 = (bf16[3,3,128,4,256]{4,2,3,1,0:T(8,128)(2,1)S(1)}, bf16[3,3,128,4,256]{4,2,3,1,0:T(8,128)(2,1)}, u32[]{:S(2)}) copy-start(bf16[3,3,128,4,256]{4,2,3,1,0:T(8,128)(2,1)} %copy.20) | copy-start | bytes 7077892
  100.7 4.4 %copy-start.2 = (bf16[1,16,14,14,256]{4,1,3,2,0:T(8,128)(2,1)S(1)}, bf16[1,16,14,14,256]{4,1,3,2,0:T(8,128)(2,1)}, u32[]{:S(2)}) copy-start(bf16[1,16,14,14,256]{4,1,3,2,0:T(8,128)(2,1)} %param.9) | copy-start | bytes 4816900
  105.0 10.1 %copy-start = (bf16[16,14,14,512]{3,0,2,1:T(8,128)(2,1)}, bf16[16,14,14,512]{3,0,2,1:T(8,128)(2,1)S(1)}, u32[]{:S(2)}) copy-start(bf16[16,14,14,512]{3,0,2,1:T(8,128)(2,1)S(1)} %copy.21) | copy-start | bytes 9633796
  115.2 232.3 %all-reduce.2.cloned.1.call-start = ((), (), s32[]{:S(2)}) async-start(), calls=%async_computation.4 | async-start | bytes 9437184 | tf_op jit(solution)/shard_map/psum | solution.py:34
  193.8 21.9 %collective-permute-start.1 = (bf16[16,14,14,128]{3,0,2,1:T(8,128)(2,1)S(1)}, bf16[16,14,14,128]{3,0,2,1:T(8,128)(2,1)S(1)}, u32[]{:S(2)}, u32[]{:S(2)}) collective-permute-start(bf16[16,14,14,128]{3,0,2,1:T(8,128)(2,1)S(1)} %fusion.5), channel_id=1, source_target_pairs={{4,0},{5,1},{6,2},{7,3},{12,8},{13,9},{14,10},{15,11},{20,16},{21,... | collective-permute-start | bytes 2408456 | tf_op jit(solution)/shard_map/ppermute | solution.py:36
Sparse Core Ops, SparseCore 0:
  30.5 53.4 all-gather.2
  115.3 49.1 all-gather.4
  176.6 170.8 all-reduce.1

commit v2 on v0

v2 whole, which is shorter than its diff:
```python
import jax
import jax.numpy as jnp
from jax import lax
from jax.experimental import pallas as pl
from jax.experimental.pallas import tpu as pltpu
from jax.sharding import PartitionSpec as P

BF = jnp.bfloat16
F32 = jnp.float32
HW = 14
NI = 16
PW = 16
CC = 128
CO = 256
CIN, COUT = 512, 1024
HC = 2
NH = HW // HC
NG = 4
GI = NI // NG
TAPS = 9
N1 = 5
N0 = TAPS - N1
LMID, LEND = 4, 9
ROWS = PW * NI
KROWS = HW * ROWS
KH = CC // 4


def copy_to(src, dst, ssem, rsem, dev):
    return pltpu.make_async_remote_copy(src, dst, ssem, rsem, device_id=dev, device_id_type=pl.DeviceIdType.MESH)


def loop(lo, hi, fn):
    def one(n, carry):
        fn(n)
        return carry

    lax.fori_loop(lo, hi, one, 0)


def body_kernel(
    act, w, sc, sh, dz, z_out, da_out, gw_out,
    IM, L, Kf, KX, Dv, AT, GP, PB, R1, R2, Kb, AC, DA, ZF,
    rA, sAy, sAx, sAc, rX, sXx, sXz, lK, sKc, rKc, lM, rG, sGx, sGc,
    rP, sP, r1, r2, s1, s2, s3, so, sU, rD, sD,
):
    z, y, t = lax.axis_index("dp"), lax.axis_index("stage"), lax.axis_index("tp")
    x, c = t // 2, t % 2
    tc = t + 1 - 2 * c
    tx = (t + 2) % NG
    txc = (tc + 2) % NG
    zp = z % 2
    dev_y, dev_x, dev_c = (z, 1 - y, t), (z, y, tx), (z, y, tc)
    dev_z = (z + 1 - 2 * zp, y, t)
    mid = (z == 1) | (z == 2)
    lag = jnp.where(mid, LMID, LEND)

    peers = [dev_x, dev_c, ((z + 1) % NG, y, t), ((z + 3) % NG, y, t)] + [(z, 1 - y, g) for g in (t, tc, tx, txc)]
    bar = pltpu.get_barrier_semaphore()
    for d in peers:
        pl.semaphore_signal(bar, 1, device_id=d, device_id_type=pl.DeviceIdType.MESH)
    pl.semaphore_wait(bar, len(peers))

    def lanes(start, size):
        return pl.ds(pl.multiple_of(start, CC), size)

    def rows(v):
        return pl.ds(HC * v, HC)

    def up1(q, p):
        return copy_to(PB.at[q, p], R1.at[q, p % N1], s1.at[q, p], r1.at[q, p], (z + 1, y, t))

    def from3(q, p):
        return copy_to(PB.at[q, p], R2.at[q, p], s1.at[q, p], r2.at[q, p], (z - 1, y, t))

    def root_lo(q, p):
        return copy_to(PB.at[q, p], R2.at[q, p], s2.at[q, p], r2.at[q, p], (z - 1, y, t))

    def root_hi(q, p):
        return copy_to(PB.at[q, p], R2.at[q, p], s3.at[q, p], r2.at[q, p], (z + 1, y, t))

    def last_lo(q, p):
        return copy_to(R2.at[q, p], R2.at[q, p], s2.at[q, p], r2.at[q, p], (z - 1, y, t))

    def reduce_end(q, p):
        @pl.when(z == 0)
        def _():
            up1(q, p).start()

        @pl.when(z == 3)
        def _():
            from3(q, p).start()

    def reduce_mid(q, p):
        @pl.when(z == 1)
        def _():
            up1(q, p).wait_recv()
            PB[q, p] = PB[q, p] + R1[q, p % N1]
            up1(q, p).start()

        @pl.when(z == 2)
        def _():
            up1(q, p).wait_recv()
            from3(q, p).wait_recv()
            PB[q, p] = PB[q, p] + R1[q, p % N1] + R2[q, p]
            root_lo(q, p).start()
            root_hi(q, p).start()

    def line_final(q, p, use):
        @pl.when(z != 2)
        def _():
            root_lo(q, p).wait_recv()

        @pl.when(z == 1)
        def _():
            last_lo(q, p).start()

        @pl.when(z == 2)
        def _():
            use(PB, q, p).start()

        @pl.when(z != 2)
        def _():
            use(R2, q, p).start()

    def line_drain(q, p):
        @pl.when(z != 2)
        def _():
            up1(q, p).wait_send()

        @pl.when(z == 2)
        def _():
            root_lo(q, p).wait_send()
            root_hi(q, p).wait_send()

        @pl.when(z == 1)
        def _():
            last_lo(q, p).wait_send()

    def down(q, p):
        return copy_to(PB.at[q, p], PB.at[q, p], sP.at[q, p], rP.at[q, p], dev_y)

    def up_final(src, q, p):
        return copy_to(src.at[q, p], R2.at[q, p], sU.at[q, p], r2.at[q, p], dev_y)

    def act_up(u):
        return copy_to(act.at[rows(u)], L.at[t, rows(u)], sAy.at[u], rA.at[t, u], dev_y)

    def da_land(src_t):
        return copy_to(
            DA.at[0], da_out.at[pl.ds(NH * (src_t % 2), NH), :, :, lanes(CO * (src_t // 2), CO)],
            sD.at[0], rD.at[src_t], dev_y)

    @pl.when(y == 0)
    def _():
        loop(0, NH, lambda u: act_up(u).start())
        ZF[...] = jnp.zeros(ZF.shape, F32)

        def zfill(n):
            return pltpu.make_async_copy(
                ZF, gw_out.at[n // NG, :, lanes(CO * (n % NG), CO)], so.at[n % NG, n // NG])

        loop(0, TAPS * NG, lambda n: zfill(n).start())

        def zero_row(h):
            Dv[h] = jnp.zeros(Dv.shape[1:], BF)

        loop(0, HW, zero_row)
        zc = pltpu.make_async_copy(Dv, z_out, lM.at[0])
        zc.start()

        def row_round(q0):
            cnt = 2 * N0

            def block(n):
                return q0 + n // N0, N1 + n % N0

            def step(n):
                @pl.when(n < cnt)
                def _():
                    q, p = block(n)
                    down(q, p).wait_recv()
                    reduce_end(q, p)
                    reduce_mid(q, p)

                @pl.when((n >= lag) & (n < cnt + lag))
                def _():
                    q, p = block(n - lag)
                    line_final(q, p, up_final)

            loop(0, cnt + LEND, step)

        row_round(0)
        row_round(2)

        def drain(n):
            q, p = n // N0, N1 + n % N0
            line_drain(q, p)
            up_final(R2, q, p).wait_send()

        loop(0, NG * N0, drain)
        loop(0, TAPS * NG, lambda n: zfill(n).wait())
        loop(0, NH, lambda u: act_up(u).wait_send())
        zc.wait()
        loop(0, NG, lambda g: da_land(g).wait_recv())

    @pl.when(y == 1)
    def _():
        def k_rows(b):
            return pl.ds(KH * b, KH)

        def kx_send(u):
            b = k_rows(2 * zp + u)
            return copy_to(w.at[:, b, lanes(2 * CO * (1 - x), 2 * CO)], KX.at[:, b, :], sXx.at[u], rX.at[2 * zp + u], dev_x)

        def kx_share(b, u):
            return copy_to(KX.at[:, k_rows(b), :], KX.at[:, k_rows(b), :], sXz.at[u], rX.at[b], dev_z)

        def kf_rows(chunk, b):
            return Kf.at[:, pl.ds(CC * chunk + KH * b, KH), :]

        def kx_mine(b):
            return pltpu.make_async_copy(KX.at[:, k_rows(b), lanes(CO * c, CO)], kf_rows(tx, b), lK.at[b])

        def kx_partner(b, chunk):
            return copy_to(KX.at[:, k_rows(b), lanes(CO * (1 - c), CO)], kf_rows(chunk, b), sKc.at[b], rKc.at[b], dev_c)

        def kx_got(b):
            kx_mine(b).start()
            kx_partner(b, tx).start()

        def kx_x(u):
            b = 2 * zp + u
            kx_share(b, u).wait_recv()
            kx_share(b, u).start()
            kx_got(b)

        def kx_z(u):
            b = 2 * (1 - zp) + u
            kx_share(b, u).wait_recv()
            kx_got(b)

        def k_part(chunk):
            return copy_to(w.at[:, :, lanes(CO * tc, CO)], Kf.at[:, pl.ds(CC * chunk, CC), :], sKc.at[4], rKc.at[4], dev_c)

        def kb_part(at):
            return copy_to(w, Kb.at[:, pl.ds(CC * at, CC), :], sKc.at[5], rKc.at[5], dev_c)

        for u in range(2):
            kx_send(u).start()
        k_own = pltpu.make_async_copy(w.at[:, :, lanes(CO * t, CO)], Kf.at[:, pl.ds(CC * t, CC), :], lK.at[4])
        k_own.start()
        k_part(t).start()
        kb_own = pltpu.make_async_copy(w, Kb.at[:, pl.ds(CC * c, CC), :], lM.at[1])
        kb_own.start()
        kb_part(c).start()
        d_load = pltpu.make_async_copy(dz, Dv, lM.at[2])
        d_load.start()

        def im_zero(h):
            IM[h, 0:2] = jnp.zeros((2, NI, CIN), BF)
            IM[h, PW:PW + 2] = jnp.zeros((2, NI, CIN), BF)

        loop(0, PW, im_zero)
        for h in (0, PW - 1):
            IM[h, 2:PW] = jnp.zeros((HW, NI, CIN), BF)
            AT[:, :, ROWS * h:ROWS * (h + 1)] = jnp.zeros((3, CC, ROWS), BF)

        def gp_zero(g):
            for h in (0, PW - 1):
                GP[g, h] = jnp.zeros((PW, NI, CO), BF)
                GP[g, :, h] = jnp.zeros((PW, NI, CO), BF)

        loop(0, NG, gp_zero)

        def a_x(u):
            return copy_to(L.at[t, rows(u)], L.at[t, rows(u)], sAx.at[u], rA.at[t, u], dev_x)

        def a_c(g, u, s):
            return copy_to(L.at[g, rows(u)], L.at[g, rows(u)], sAc.at[s, u], rA.at[g, u], dev_c)

        def a_wait(g, u):
            a_c(g, u, 0).wait_recv()

        def own_arrive(u):
            a_wait(t, u)
            a_x(u).start()
            a_c(t, u, 0).start()

        def x_arrive(u):
            a_wait(tx, u)
            a_c(tx, u, 1).start()

        def assemble(u):
            a_wait(tc, u)
            a_wait(txc, u)
            for hh in range(HC):
                h = HC * u + hh
                IM[h + 1, 2:PW] = jnp.concatenate([L[g, h] for g in range(NG)], axis=1)
                for j in range(3):
                    blk = IM[h + 1, j:j + PW, :, lanes(CC * t, CC)]
                    AT[j, :, pl.ds(pl.multiple_of(ROWS * (h + 1), ROWS), ROWS)] = blk.reshape(ROWS, CC).T

        def g_rows(co, v):
            return GP.at[co, pl.ds(HC * v + 1, HC), pl.ds(1, HW)]

        def g_x(v):
            return copy_to(g_rows(t, v), g_rows(t, v), sGx.at[v], rG.at[t, v], dev_x)

        def g_c(co, v, s):
            return copy_to(g_rows(co, v), g_rows(co, v), sGc.at[s, v], rG.at[co, v], dev_c)

        def g_wait(co, v):
            g_c(co, v, 0).wait_recv()

        scv, shv = sc[...].reshape(1, 1, 1, CO), sh[...].reshape(1, 1, 1, CO)

        def forward(v):
            def lhs(hh):
                return jnp.concatenate(
                    [IM[HC * v + hh + i, j + 1:j + 1 + HW].reshape(HW * NI, CIN) for i in range(3) for j in range(3)],
                    axis=1)

            pre = jnp.dot(
                jnp.concatenate([lhs(hh) for hh in range(HC)], axis=0),
                Kf[...].reshape(TAPS * CIN, CO), preferred_element_type=F32)
            lin = pre.reshape(HC, HW, NI, CO) * scv + shv
            dv = Dv[rows(v)].astype(F32)
            GP[t, pl.ds(HC * v + 1, HC), 1:1 + HW] = jnp.where(lin > 0, dv * scv, 0.0).astype(BF)
            Dv[rows(v)] = jnp.maximum(lin, 0.0).astype(BF)
            g_x(v).start()
            g_c(t, v, 0).start()

        own_arrive(0)
        own_arrive(1)
        kx_x(0)
        own_arrive(2)
        own_arrive(3)
        kx_x(1)
        own_arrive(4)
        own_arrive(5)
        kx_z(0)
        own_arrive(6)
        x_arrive(0)
        kx_z(1)
        x_arrive(1)
        assemble(0)
        x_arrive(2)
        assemble(1)
        k_own.wait()
        k_part(tc).wait_recv()
        for b in range(NG):
            kx_mine(b).wait()
            kx_partner(b, txc).wait_recv()
        d_load.wait()

        def pipe(u):
            @pl.when(u < NH)
            def _():
                x_arrive(u)

            assemble(u - 1)
            forward(u - 2)

        forward(0)
        loop(3, NH + 1, pipe)
        forward(NH - 1)
        zc = pltpu.make_async_copy(Dv, z_out, lM.at[0])
        zc.start()

        def gw_chunk(q, co):
            def part(j):
                lhs = jnp.concatenate([AT[j, :, ROWS * i:ROWS * i + KROWS] for i in range(3)], axis=0)
                r = jnp.dot(lhs, GP[co, 1:1 + HW].reshape(KROWS, CO), preferred_element_type=F32)
                for i in range(3):
                    PB[q, 3 * j + i] = r[CC * i:CC * (i + 1)]

            loop(0, 3, part)
            loop(0, N1, lambda p: reduce_end(q, p))
            loop(N1, TAPS, lambda p: down(q, p).start())

        def chunk_of(q):
            return (t + 2 * (q // 2) + (1 - 2 * c) * (q % 2) + NG) % NG

        def out_copy(src, q, p):
            tap = 3 * (p % 3) + p // 3
            return pltpu.make_async_copy(src.at[q, p], gw_out.at[tap, :, lanes(CO * chunk_of(q), CO)], so.at[q, p])

        def step(n):
            @pl.when(n < NG * N1)
            def _():
                reduce_mid(n // N1, n % N1)

            @pl.when((n >= lag) & (n < NG * N1 + lag))
            def _():
                m = n - lag
                line_final(m // N1, m % N1, out_copy)

        def da_tap(tap):
            i, j = tap // 3, tap % 3
            lhs = jnp.concatenate(
                [
                    GP[g, pl.ds(NH * c + 2 - i, NH), pl.ds(2 - j, HW)].reshape(NH * HW * NI, CO)
                    for g in range(NG)
                ],
                axis=1)
            return lax.dot_general(lhs, Kb[tap], (((1,), (1,)), ((), ())), preferred_element_type=F32)

        def da_send(g):
            return copy_to(
                DA.at[g], da_out.at[pl.ds(NH * c, NH), :, :, lanes(CO * x, CO)], sD.at[g], rD.at[t], (z, 0, g))

        gw_chunk(0, t)
        loop(0, NH, lambda v: g_wait(tc, v))
        gw_chunk(1, tc)

        def relay(v):
            g_wait(tx, v)
            g_c(tx, v, 1).start()

        n = 0
        for v in range(NH):
            relay(v)
            stop = n + 1 + v % 2
            loop(n, stop, step)
            n = stop
        gw_chunk(2, tx)
        loop(0, NH, lambda v: g_wait(txc, v))
        gw_chunk(3, txc)
        kb_own.wait()
        kb_part(1 - c).wait_recv()
        AC[...] = da_tap(0)

        def da_step(k):
            step(n + k - 1)
            AC[...] += da_tap(k)

        loop(1, TAPS, da_step)
        n = n + TAPS - 1
        for g in range(NG):
            DA[g] = AC[...].reshape(NH, HW, NI, CO)[:, :, GI * g:GI * (g + 1), :].astype(BF)
            da_send(g).start()
        loop(n, NG * N1 + LEND, step)

        def detour(m):
            q, p = m // N0, N1 + m % N0
            up_final(R2, q, p).wait_recv()
            out_copy(R2, q, p).start()

        loop(0, NG * N0, detour)

        for u in range(2):
            kx_send(u).wait_send()
            kx_share(2 * zp + u, u).wait_send()
        for b in range(NG):
            kx_partner(b, tx).wait_send()
        k_part(t).wait_send()
        kb_part(c).wait_send()

        def drain_a(u):
            a_x(u).wait_send()
            a_c(t, u, 0).wait_send()
            a_c(tx, u, 1).wait_send()
            g_x(u).wait_send()
            g_c(t, u, 0).wait_send()
            g_c(tx, u, 1).wait_send()

        loop(0, NH, drain_a)
        L[0] = jnp.zeros(L.shape[1:], BF)
        zeros = pltpu.make_async_copy(L.at[0], da_out, lM.at[3])
        zeros.start()
        loop(0, NG * N1, lambda m: line_drain(m // N1, m % N1))
        loop(0, NG * N0, lambda m: down(m // N0, N1 + m % N0).wait_send())
        loop(0, TAPS * NG, lambda m: out_copy(R2, m // TAPS, m % TAPS).wait())
        loop(0, NG, lambda g: da_send(g).wait_send())
        zc.wait()
        zeros.wait()


def solution(mesh):
    def body(act_loc, w_loc, scale_loc, shift_loc, grad_loc):
        dma = pltpu.SemaphoreType.DMA
        hbm = pl.BlockSpec(memory_space=pl.ANY)
        vmem = pl.BlockSpec(memory_space=pltpu.VMEM)
        block = (NG, TAPS)
        scratch = [
            pltpu.VMEM((PW, PW + 2, NI, CIN), BF),
            pltpu.VMEM((NG, HW, HW, GI, CIN), BF),
            pltpu.VMEM((TAPS, CIN, CO), BF),
            pltpu.VMEM((TAPS, CC, 2 * CO), BF),
            pltpu.VMEM((HW, HW, NI, CO), BF),
            pltpu.VMEM((3, CC, PW * ROWS), BF),
            pltpu.VMEM((NG, PW, PW, NI, CO), BF),
            pltpu.VMEM(block + (CC, CO), F32),
            pltpu.VMEM((NG, N1, CC, CO), F32),
            pltpu.VMEM(block + (CC, CO), F32),
            pltpu.VMEM((TAPS, 2 * CC, COUT), BF),
            pltpu.VMEM((NH * HW * NI, CO), F32),
            pltpu.VMEM((NG, NH, HW, GI, CO), BF),
            pltpu.VMEM((CC, CO), F32),
            dma((NG, NH)), dma((NH,)), dma((NH,)), dma((2, NH)),
            dma((4,)), dma((2,)), dma((2,)), dma((5,)), dma((6,)), dma((6,)), dma((4,)),
            dma((NG, NH)), dma((NH,)), dma((2, NH)),
        ] + [dma(block)] * 9 + [dma((NG,)), dma((NG,))]
        act = jnp.transpose(act_loc[0], (1, 2, 0, 3))
        dz = jnp.transpose(grad_loc[0], (1, 2, 0, 3))
        z_blk, da, gw = pl.pallas_call(
            body_kernel,
            out_shape=[
                jax.ShapeDtypeStruct((HW, HW, NI, CO), BF),
                jax.ShapeDtypeStruct((HW, HW, GI, CIN), BF),
                jax.ShapeDtypeStruct((TAPS, CC, COUT), F32),
            ],
            in_specs=[hbm, hbm, vmem, vmem, hbm],
            out_specs=[hbm, hbm, hbm],
            scratch_shapes=scratch,
            compiler_params=pltpu.CompilerParams(collective_id=0, has_side_effects=True, vmem_limit_bytes=62 * 2**20),
            name="stage_conv",
        )(act, w_loc[0].reshape(TAPS, CC, COUT), scale_loc, shift_loc, dz)
        back = (2, 0, 1, 3)
        return jnp.transpose(z_blk, back)[None], jnp.transpose(da, back)[None], gw.reshape(1, 3, 3, CC, COUT)

    act_spec = P("stage", ("dp", "tp"))
    w_spec = P("stage", None, None, "tp")
    vec_spec = P("stage", "tp")
    grad_spec = P("stage", "dp", None, None, "tp")
    return jax.shard_map(body, mesh=mesh, in_specs=(act_spec, w_spec, vec_spec, vec_spec, grad_spec), out_specs=(grad_spec, act_spec, w_spec), check_vma=False)
```

time: 469 us -> 148 us (0.32)
  waiting for transfers between devices: 299 us -> 0 us
  Pallas kernels: 0 us -> 139 us
  local copies, waits for them, and re-layouts: 73 us -> 7.32 us
  matrix products: 40.4 us -> 0 us
  blocking collectives: 31.3 us -> 0 us
  between operations: 13.8 us -> 0.65 us
  starting transfers between devices: 5.53 us -> 0 us
  other arithmetic: 5.04 us -> 0 us
    pallas_call x0 -> x1, Pallas kernels: none -> 139 us  [body(): pl.pallas_call(body_kernel, out_shape=[jax.ShapeDtypeStruct((HW, HW, NI,...]
    psum x1 -> x0, waiting for transfers between devices: 114 us -> none  [body(): dw_blk = lax.psum(dw_part, 'dp')]
    reduce_scatter x1 -> x0, waiting for transfers between devices: 99.1 us -> none  [body(): pre_out = lax.psum_scatter(part_sum, 'tp', scatter_dimension=3, tiled=True)]
    unnamed x15 -> x5, local copies, waits for them, and re-layouts: 60.1 us -> 7.32 us
    all_gather x1 -> x0, waiting for transfers between devices: 48.1 us -> none  [body(): grad_full = lax.all_gather(grad_blk, 'tp', axis=3, tiled=True)]
    conv_general_dilated x3 -> x0, matrix products: 40.4 us -> none  [the longest x1 17.3 us: conv_input_grad(): lax.conv_general_dilated(grad_out, kernel[::-1, ::-1], (1, 1), 'SAME', di...]
    ppermute x2 -> x0, waiting for transfers between devices: 37.8 us -> none  [the longest x1 20.6 us: body(): dact_back = lax.ppermute(dact_blk, 'stage', perm=[(1, 0)])]
    all_to_all x2 -> x0, blocking collectives: 31.3 us -> none  [the longest x1 15.9 us: body(): moved = lax.all_to_all(images, 'tp', 3, 0, tiled=True)]
  transfers between devices with their start and end apart: 5 -> 0, of which waited for: 5 -> 0; matrix products, arithmetic and copies ran while one was open for 4% -> 0% of each run, Pallas kernels for 0% -> 0%
where the time goes in v2:
time: 148 us; the launch traced here: 147 us
  Pallas kernels  139 us (94%)
  local copies, waits for them, and re-layouts  7.32 us (5%)
    pallas_call x1, Pallas kernels, body(): pl.pallas_call(body_kernel, out_shape=[jax.ShapeDtypeStruct((HW, HW, NI,...  139 us
    unnamed x5, local copies, waits for them, and re-layouts  7.32 us

profile of v2, /device:TPU:0, one launch (start us, length us, event | category | flops | bytes accessed | tf_op | source)
XLA Modules:
  0.0 146.9 jit_solution(3901369639169018746)
XLA Ops:
  0.6 138.9 %stage_conv.1 = (bf16[14,14,16,256]{3,2,1,0:T(8,128)(2,1)}, bf16[14,14,4,512]{3,2,1,0:T(4,128)(2,1)}, f32[9,128,1024]{2,1,0:T(8,128)}) custom-call(bf16[14,14,4,512]{3,2,1,0:T(4,128)(2,1)} %bitcast.19, bf16[9,128,1024]{2,1,0:T(8,128)(2,1)} %bitcast.15, f32[1,256]{1,0:T(1,128)} %sc.1, f32[1,256]{1,0:T(1,128)} %sh.1, bf16[14,14,16,256]{3,2,1,0:T(8,128)(2,1)} %bitcast.16), custom_call_target="tpu_custom_call" | custom-call | tf_op jit(solution)/shard_map/stage_conv/pallas_call | solution.py:507
  139.6 0.0 copy-start
  139.6 2.8 %copy.11 = bf16[1,16,14,14,256]{4,1,3,2,0:T(8,128)(2,1)} copy(bf16[1,16,14,14,256]{4,1,3,2,0:T(8,128)(2,1)} %bitcast.17) | data formatting | bytes 3211264
  142.4 2.3 %copy.12 = bf16[1,4,14,14,512]{4,1,3,2,0:T(4,128)(2,1)} copy(bf16[1,4,14,14,512]{4,1,3,2,0:T(4,128)(2,1)} %bitcast.18) | data formatting | bytes 1605632
  144.7 0.0 copy-done
  144.7 2.2 %copy.13 = f32[1,3,3,128,1024]{4,3,2,1,0:T(8,128)} copy(f32[1,3,3,128,1024]{4,3,2,1,0:T(8,128)S(1)} %bitcast.14) | data formatting | bytes 9437184
Async XLA Ops:
  139.6 5.1 %copy-start = (f32[9,128,1024]{2,1,0:T(8,128)S(1)}, f32[9,128,1024]{2,1,0:T(8,128)}, u32[]{:S(2)}) copy-start(f32[9,128,1024]{2,1,0:T(8,128)} %get-tuple-element.8) | copy-start | bytes 14155780

commit v3 on v2

--- a/solution.py
+++ b/solution.py
@@ -18,12 +18,16 @@
 NG = 4
 GI = NI // NG
 TAPS = 9
-N1 = 5
-N0 = TAPS - N1
+NA, NB = 5, 6
+NROW = 2 * NA + 2 * NB
+NDET = NG * TAPS - NROW
 LMID, LEND = 4, 9
 ROWS = PW * NI
 KROWS = HW * ROWS
-KH = CC // 4
+KH = 16
+KP = CC // KH
+KHALF = KP // 2
+UX = 3
 
 
 def copy_to(src, dst, ssem, rsem, dev):
@@ -67,8 +71,19 @@
     def rows(v):
         return pl.ds(HC * v, HC)
 
+    def row_block(n):
+        m = n - 2 * NA
+        late = m >= 0
+        return jnp.where(late, 2 + m // NB, n // NA), jnp.where(late, m % NB, n % NA)
+
+    def detour_block(n):
+        m = n - 2 * (TAPS - NA)
+        late = m >= 0
+        lo, hi = TAPS - NA, TAPS - NB
+        return jnp.where(late, 2 + m // hi, n // lo), jnp.where(late, NB + m % hi, NA + n % lo)
+
     def up1(q, p):
-        return copy_to(PB.at[q, p], R1.at[q, p % N1], s1.at[q, p], r1.at[q, p], (z + 1, y, t))
+        return copy_to(PB.at[q, p], R1.at[q, p % NB], s1.at[q, p], r1.at[q, p], (z + 1, y, t))
 
     def from3(q, p):
         return copy_to(PB.at[q, p], R2.at[q, p], s1.at[q, p], r2.at[q, p], (z - 1, y, t))
@@ -95,14 +110,14 @@
         @pl.when(z == 1)
         def _():
             up1(q, p).wait_recv()
-            PB[q, p] = PB[q, p] + R1[q, p % N1]
+            PB[q, p] = PB[q, p] + R1[q, p % NB]
             up1(q, p).start()
 
         @pl.when(z == 2)
         def _():
             up1(q, p).wait_recv()
             from3(q, p).wait_recv()
-            PB[q, p] = PB[q, p] + R1[q, p % N1] + R2[q, p]
+            PB[q, p] = PB[q, p] + R1[q, p % NB] + R2[q, p]
             root_lo(q, p).start()
             root_hi(q, p).start()
 
@@ -145,6 +160,12 @@
 
     def act_up(u):
         return copy_to(act.at[rows(u)], L.at[t, rows(u)], sAy.at[u], rA.at[t, u], dev_y)
+
+    def act_cross(src_t, u):
+        return copy_to(act.at[rows(u)], L.at[src_t, rows(u)], sAx.at[u], rA.at[src_t, u], dev_x)
+
+    def act_relay(u):
+        return copy_to(L.at[tx, rows(u)], L.at[tx, rows(u)], sAc.at[0, u], rA.at[tx, u], dev_y)
 
     def da_land(src_t):
         return copy_to(
@@ -153,7 +174,15 @@
 
     @pl.when(y == 0)
     def _():
-        loop(0, NH, lambda u: act_up(u).start())
+        loop(UX, NH, lambda u: act_up(u).start())
+        loop(0, UX, lambda u: act_cross(t, u).start())
+
+        def raise_rows(u):
+            act_up(u).start()
+            act_cross(tx, u).wait_recv()
+            act_relay(u).start()
+
+        loop(0, UX, raise_rows)
         ZF[...] = jnp.zeros(ZF.shape, F32)
 
         def zfill(n):
@@ -169,38 +198,35 @@
         zc = pltpu.make_async_copy(Dv, z_out, lM.at[0])
         zc.start()
 
-        def row_round(q0):
-            cnt = 2 * N0
-
-            def block(n):
-                return q0 + n // N0, N1 + n % N0
-
+        def row_round(lo, hi):
             def step(n):
-                @pl.when(n < cnt)
+                @pl.when(n < hi)
                 def _():
-                    q, p = block(n)
+                    q, p = detour_block(n)
                     down(q, p).wait_recv()
                     reduce_end(q, p)
                     reduce_mid(q, p)
 
-                @pl.when((n >= lag) & (n < cnt + lag))
+                @pl.when((n >= lo + lag) & (n < hi + lag))
                 def _():
-                    q, p = block(n - lag)
+                    q, p = detour_block(n - lag)
                     line_final(q, p, up_final)
 
-            loop(0, cnt + LEND, step)
-
-        row_round(0)
-        row_round(2)
+            loop(lo, hi + LEND, step)
+
+        row_round(0, 2 * (TAPS - NA))
+        row_round(2 * (TAPS - NA), NDET)
 
         def drain(n):
-            q, p = n // N0, N1 + n % N0
+            q, p = detour_block(n)
             line_drain(q, p)
             up_final(R2, q, p).wait_send()
 
-        loop(0, NG * N0, drain)
+        loop(0, NDET, drain)
         loop(0, TAPS * NG, lambda n: zfill(n).wait())
         loop(0, NH, lambda u: act_up(u).wait_send())
+        loop(0, UX, lambda u: act_cross(t, u).wait_send())
+        loop(0, UX, lambda u: act_relay(u).wait_send())
         zc.wait()
         loop(0, NG, lambda g: da_land(g).wait_recv())
 
@@ -210,8 +236,8 @@
             return pl.ds(KH * b, KH)
 
         def kx_send(u):
-            b = k_rows(2 * zp + u)
-            return copy_to(w.at[:, b, lanes(2 * CO * (1 - x), 2 * CO)], KX.at[:, b, :], sXx.at[u], rX.at[2 * zp + u], dev_x)
+            b = k_rows(KHALF * zp + u)
+            return copy_to(w.at[:, b, lanes(2 * CO * (1 - x), 2 * CO)], KX.at[:, b, :], sXx.at[u], rX.at[KHALF * zp + u], dev_x)
 
         def kx_share(b, u):
             return copy_to(KX.at[:, k_rows(b), :], KX.at[:, k_rows(b), :], sXz.at[u], rX.at[b], dev_z)
@@ -230,25 +256,24 @@
             kx_partner(b, tx).start()
 
         def kx_x(u):
-            b = 2 * zp + u
+            b = KHALF * zp + u
             kx_share(b, u).wait_recv()
             kx_share(b, u).start()
             kx_got(b)
 
         def kx_z(u):
-            b = 2 * (1 - zp) + u
+            b = KHALF * (1 - zp) + u
             kx_share(b, u).wait_recv()
             kx_got(b)
 
         def k_part(chunk):
-            return copy_to(w.at[:, :, lanes(CO * tc, CO)], Kf.at[:, pl.ds(CC * chunk, CC), :], sKc.at[4], rKc.at[4], dev_c)
+            return copy_to(w.at[:, :, lanes(CO * tc, CO)], Kf.at[:, pl.ds(CC * chunk, CC), :], sKc.at[KP], rKc.at[KP], dev_c)
 
         def kb_part(at):
-            return copy_to(w, Kb.at[:, pl.ds(CC * at, CC), :], sKc.at[5], rKc.at[5], dev_c)
-
-        for u in range(2):
-            kx_send(u).start()
-        k_own = pltpu.make_async_copy(w.at[:, :, lanes(CO * t, CO)], Kf.at[:, pl.ds(CC * t, CC), :], lK.at[4])
+            return copy_to(w, Kb.at[:, pl.ds(CC * at, CC), :], sKc.at[KP + 1], rKc.at[KP + 1], dev_c)
+
+        loop(0, KHALF, lambda u: kx_send(u).start())
+        k_own = pltpu.make_async_copy(w.at[:, :, lanes(CO * t, CO)], Kf.at[:, pl.ds(CC * t, CC), :], lK.at[KP])
         k_own.start()
         k_part(t).start()
         kb_own = pltpu.make_async_copy(w, Kb.at[:, pl.ds(CC * c, CC), :], lM.at[1])
@@ -284,7 +309,8 @@
 
         def own_arrive(u):
             a_wait(t, u)
-            a_x(u).start()
+            if u >= UX:
+                a_x(u).start()
             a_c(t, u, 0).start()
 
         def x_arrive(u):
@@ -331,53 +357,72 @@
             g_x(v).start()
             g_c(t, v, 0).start()
 
-        own_arrive(0)
-        own_arrive(1)
+        own_arrive(3)
         kx_x(0)
-        own_arrive(2)
-        own_arrive(3)
+        own_arrive(4)
         kx_x(1)
-        own_arrive(4)
         own_arrive(5)
         kx_z(0)
         own_arrive(6)
+        kx_x(2)
+        kx_z(1)
+        own_arrive(0)
+        kx_x(3)
         x_arrive(0)
-        kx_z(1)
-        x_arrive(1)
+        kx_z(2)
+        x_arrive(3)
+        own_arrive(1)
+        x_arrive(4)
+        kx_z(3)
+        assemble(3)
         assemble(0)
-        x_arrive(2)
-        assemble(1)
         k_own.wait()
         k_part(tc).wait_recv()
-        for b in range(NG):
+
+        def k_ready(b):
             kx_mine(b).wait()
             kx_partner(b, txc).wait_recv()
+
+        loop(0, KP, k_ready)
         d_load.wait()
-
-        def pipe(u):
-            @pl.when(u < NH)
-            def _():
-                x_arrive(u)
-
-            assemble(u - 1)
-            forward(u - 2)
-
+        x_arrive(1)
+        assemble(4)
+        assemble(1)
         forward(0)
-        loop(3, NH + 1, pipe)
-        forward(NH - 1)
+        x_arrive(5)
+        assemble(5)
+        own_arrive(2)
+        forward(4)
+        x_arrive(6)
+        assemble(6)
+        x_arrive(2)
+        loop(5, NH, forward)
+        assemble(2)
+        forward(3)
+        loop(1, 3, forward)
         zc = pltpu.make_async_copy(Dv, z_out, lM.at[0])
         zc.start()
 
         def gw_chunk(q, co):
-            def part(j):
+            mine = NA if q < 2 else NB
+
+            def part(k):
+                j = k if q < 2 else (k + 2) % 3
                 lhs = jnp.concatenate([AT[j, :, ROWS * i:ROWS * i + KROWS] for i in range(3)], axis=0)
                 r = jnp.dot(lhs, GP[co, 1:1 + HW].reshape(KROWS, CO), preferred_element_type=F32)
                 for i in range(3):
-                    PB[q, 3 * j + i] = r[CC * i:CC * (i + 1)]
+                    p = 3 * j + i
+                    PB[q, p] = r[CC * i:CC * (i + 1)]
+
+                    @pl.when(p < mine)
+                    def _():
+                        reduce_end(q, p)
+
+                    @pl.when(p >= mine)
+                    def _():
+                        down(q, p).start()
 
             loop(0, 3, part)
-            loop(0, N1, lambda p: reduce_end(q, p))
-            loop(N1, TAPS, lambda p: down(q, p).start())
 
         def chunk_of(q):
             return (t + 2 * (q // 2) + (1 - 2 * c) * (q % 2) + NG) % NG
@@ -387,14 +432,14 @@
             return pltpu.make_async_copy(src.at[q, p], gw_out.at[tap, :, lanes(CO * chunk_of(q), CO)], so.at[q, p])
 
         def step(n):
-            @pl.when(n < NG * N1)
+            @pl.when(n < NROW)
             def _():
-                reduce_mid(n // N1, n % N1)
-
-            @pl.when((n >= lag) & (n < NG * N1 + lag))
+                reduce_mid(*row_block(n))
+
+            @pl.when((n >= lag) & (n < NROW + lag))
             def _():
-                m = n - lag
-                line_final(m // N1, m % N1, out_copy)
+                q, p = row_block(n - lag)
+                line_final(q, p, out_copy)
 
         def da_tap(tap):
             i, j = tap // 3, tap % 3
@@ -419,10 +464,10 @@
             g_c(tx, v, 1).start()
 
         n = 0
-        for v in range(NH):
+        for v, stop in zip((0, 4, 5, 6, 3, 1, 2), (0, 0, 1, 3, 5, 7, 8)):
             relay(v)
-            stop = n + 1 + v % 2
-            loop(n, stop, step)
+            if stop > n:
+                loop(n, stop, step)
             n = stop
         gw_chunk(2, tx)
         loop(0, NH, lambda v: g_wait(txc, v))
@@ -440,25 +485,22 @@
         for g in range(NG):
             DA[g] = AC[...].reshape(NH, HW, NI, CO)[:, :, GI * g:GI * (g + 1), :].astype(BF)
             da_send(g).start()
-        loop(n, NG * N1 + LEND, step)
+        loop(n, NROW + LEND, step)
 
         def detour(m):
-            q, p = m // N0, N1 + m % N0
+            q, p = detour_block(m)
             up_final(R2, q, p).wait_recv()
             out_copy(R2, q, p).start()
 
-        loop(0, NG * N0, detour)
-
-        for u in range(2):
-            kx_send(u).wait_send()
-            kx_share(2 * zp + u, u).wait_send()
-        for b in range(NG):
-            kx_partner(b, tx).wait_send()
+        loop(0, NDET, detour)
+
+        loop(0, KHALF, lambda u: kx_send(u).wait_send())
+        loop(0, KHALF, lambda u: kx_share(KHALF * zp + u, u).wait_send())
+        loop(0, KP, lambda b: kx_partner(b, tx).wait_send())
         k_part(t).wait_send()
         kb_part(c).wait_send()
 
         def drain_a(u):
-            a_x(u).wait_send()
             a_c(t, u, 0).wait_send()
             a_c(tx, u, 1).wait_send()
             g_x(u).wait_send()
@@ -466,11 +508,12 @@
             g_c(tx, u, 1).wait_send()
 
         loop(0, NH, drain_a)
+        loop(UX, NH, lambda u: a_x(u).wait_send())
         L[0] = jnp.zeros(L.shape[1:], BF)
         zeros = pltpu.make_async_copy(L.at[0], da_out, lM.at[3])
         zeros.start()
-        loop(0, NG * N1, lambda m: line_drain(m // N1, m % N1))
-        loop(0, NG * N0, lambda m: down(m // N0, N1 + m % N0).wait_send())
+        loop(0, NROW, lambda m: line_drain(*row_block(m)))
+        loop(0, NDET, lambda m: down(*detour_block(m)).wait_send())
         loop(0, TAPS * NG, lambda m: out_copy(R2, m // TAPS, m % TAPS).wait())
         loop(0, NG, lambda g: da_send(g).wait_send())
         zc.wait()
@@ -492,14 +535,14 @@
             pltpu.VMEM((3, CC, PW * ROWS), BF),
             pltpu.VMEM((NG, PW, PW, NI, CO), BF),
             pltpu.VMEM(block + (CC, CO), F32),
-            pltpu.VMEM((NG, N1, CC, CO), F32),
+            pltpu.VMEM((NG, NB, CC, CO), F32),
             pltpu.VMEM(block + (CC, CO), F32),
             pltpu.VMEM((TAPS, 2 * CC, COUT), BF),
             pltpu.VMEM((NH * HW * NI, CO), F32),
             pltpu.VMEM((NG, NH, HW, GI, CO), BF),
             pltpu.VMEM((CC, CO), F32),
             dma((NG, NH)), dma((NH,)), dma((NH,)), dma((2, NH)),
-            dma((4,)), dma((2,)), dma((2,)), dma((5,)), dma((6,)), dma((6,)), dma((4,)),
+            dma((KP,)), dma((KHALF,)), dma((KHALF,)), dma((KP + 1,)), dma((KP + 2,)), dma((KP + 2,)), dma((4,)),
             dma((NG, NH)), dma((NH,)), dma((2, NH)),
         ] + [dma(block)] * 9 + [dma((NG,)), dma((NG,))]
         act = jnp.transpose(act_loc[0], (1, 2, 0, 3))

time: 148 us -> 142 us (0.959)
  the two profiles are of different devices: /device:TPU:0 before, /device:TPU:6 now
where the time goes in v3:
time: 142 us
  Pallas kernels  134 us (94%)
  local copies, waits for them, and re-layouts  7.32 us (5%)
    pallas_call x1, Pallas kernels, body(): pl.pallas_call(body_kernel, out_shape=[jax.ShapeDtypeStruct((HW, HW, NI,...  134 us
    unnamed x5, local copies, waits for them, and re-layouts  7.32 us

profile of v3, /device:TPU:6, one launch (start us, length us, event | category | flops | bytes accessed | tf_op | source)
XLA Modules:
  0.0 142.0 jit_solution(160950505491708352)
XLA Ops:
  0.6 134.0 %stage_conv.1 = (bf16[14,14,16,256]{3,2,1,0:T(8,128)(2,1)}, bf16[14,14,4,512]{3,2,1,0:T(4,128)(2,1)}, f32[9,128,1024]{2,1,0:T(8,128)}) custom-call(bf16[14,14,4,512]{3,2,1,0:T(4,128)(2,1)} %bitcast.19, bf16[9,128,1024]{2,1,0:T(8,128)(2,1)} %bitcast.15, f32[1,256]{1,0:T(1,128)} %sc.1, f32[1,256]{1,0:T(1,128)} %sh.1, bf16[14,14,16,256]{3,2,1,0:T(8,128)(2,1)} %bitcast.16), custom_call_target="tpu_custom_call" | custom-call | tf_op jit(solution)/shard_map/stage_conv/pallas_call | solution.py:550
  134.7 0.0 copy-start
  134.7 2.8 %copy.11 = bf16[1,16,14,14,256]{4,1,3,2,0:T(8,128)(2,1)} copy(bf16[1,16,14,14,256]{4,1,3,2,0:T(8,128)(2,1)} %bitcast.17) | data formatting | bytes 3211264
  137.5 2.3 %copy.12 = bf16[1,4,14,14,512]{4,1,3,2,0:T(4,128)(2,1)} copy(bf16[1,4,14,14,512]{4,1,3,2,0:T(4,128)(2,1)} %bitcast.18) | data formatting | bytes 1605632
  139.8 0.0 copy-done
  139.8 2.2 %copy.13 = f32[1,3,3,128,1024]{4,3,2,1,0:T(8,128)} copy(f32[1,3,3,128,1024]{4,3,2,1,0:T(8,128)S(1)} %bitcast.14) | data formatting | bytes 9437184
Async XLA Ops:
  134.7 5.1 %copy-start = (f32[9,128,1024]{2,1,0:T(8,128)S(1)}, f32[9,128,1024]{2,1,0:T(8,128)}, u32[]{:S(2)}) copy-start(f32[9,128,1024]{2,1,0:T(8,128)} %get-tuple-element.8) | copy-start | bytes 14155780

commit v4 on v3

--- a/solution.py
+++ b/solution.py
@@ -18,10 +18,10 @@
 NG = 4
 GI = NI // NG
 TAPS = 9
-NA, NB = 5, 6
+NA, NB = 5, 5
 NROW = 2 * NA + 2 * NB
 NDET = NG * TAPS - NROW
-LMID, LEND = 4, 9
+LMID, LEND, LEND0 = 3, 8, 6
 ROWS = PW * NI
 KROWS = HW * ROWS
 KH = 16
@@ -74,13 +74,13 @@
     def row_block(n):
         m = n - 2 * NA
         late = m >= 0
-        return jnp.where(late, 2 + m // NB, n // NA), jnp.where(late, m % NB, n % NA)
+        return jnp.where(late, 2 + m // NB, n // NA), jnp.where(late, (m + 3) % NB, n % NA)
 
     def detour_block(n):
         m = n - 2 * (TAPS - NA)
         late = m >= 0
         lo, hi = TAPS - NA, TAPS - NB
-        return jnp.where(late, 2 + m // hi, n // lo), jnp.where(late, NB + m % hi, NA + n % lo)
+        return jnp.where(late, 2 + m // hi, n // lo), jnp.where(late, NB + (m + 1) % hi, NA + n % lo)
 
     def up1(q, p):
         return copy_to(PB.at[q, p], R1.at[q, p % NB], s1.at[q, p], r1.at[q, p], (z + 1, y, t))
@@ -174,15 +174,15 @@
 
     @pl.when(y == 0)
     def _():
-        loop(UX, NH, lambda u: act_up(u).start())
-        loop(0, UX, lambda u: act_cross(t, u).start())
+        loop(0, UX, lambda u: act_up(u).start())
+        loop(UX, NH, lambda u: act_cross(t, u).start())
 
         def raise_rows(u):
             act_up(u).start()
             act_cross(tx, u).wait_recv()
             act_relay(u).start()
 
-        loop(0, UX, raise_rows)
+        loop(UX, NH, raise_rows)
         ZF[...] = jnp.zeros(ZF.shape, F32)
 
         def zfill(n):
@@ -198,24 +198,22 @@
         zc = pltpu.make_async_copy(Dv, z_out, lM.at[0])
         zc.start()
 
-        def row_round(lo, hi):
-            def step(n):
-                @pl.when(n < hi)
-                def _():
-                    q, p = detour_block(n)
-                    down(q, p).wait_recv()
-                    reduce_end(q, p)
-                    reduce_mid(q, p)
-
-                @pl.when((n >= lo + lag) & (n < hi + lag))
-                def _():
-                    q, p = detour_block(n - lag)
-                    line_final(q, p, up_final)
-
-            loop(lo, hi + LEND, step)
-
-        row_round(0, 2 * (TAPS - NA))
-        row_round(2 * (TAPS - NA), NDET)
+        lag0 = jnp.where(mid, LMID, LEND0)
+
+        def step0(n):
+            @pl.when(n < NDET)
+            def _():
+                q, p = detour_block(n)
+                down(q, p).wait_recv()
+                reduce_end(q, p)
+                reduce_mid(q, p)
+
+            @pl.when((n >= lag0) & (n < NDET + lag0))
+            def _():
+                q, p = detour_block(n - lag0)
+                line_final(q, p, up_final)
+
+        loop(0, NDET + LEND0, step0)
 
         def drain(n):
             q, p = detour_block(n)
@@ -225,8 +223,8 @@
         loop(0, NDET, drain)
         loop(0, TAPS * NG, lambda n: zfill(n).wait())
         loop(0, NH, lambda u: act_up(u).wait_send())
-        loop(0, UX, lambda u: act_cross(t, u).wait_send())
-        loop(0, UX, lambda u: act_relay(u).wait_send())
+        loop(UX, NH, lambda u: act_cross(t, u).wait_send())
+        loop(UX, NH, lambda u: act_relay(u).wait_send())
         zc.wait()
         loop(0, NG, lambda g: da_land(g).wait_recv())
 
@@ -309,7 +307,7 @@
 
         def own_arrive(u):
             a_wait(t, u)
-            if u >= UX:
+            if u < UX:
                 a_x(u).start()
             a_c(t, u, 0).start()
 
@@ -357,25 +355,29 @@
             g_x(v).start()
             g_c(t, v, 0).start()
 
+        own_arrive(0)
+        kx_x(0)
+        own_arrive(1)
+        kx_x(1)
+        own_arrive(2)
+        kx_z(0)
+        kx_x(2)
         own_arrive(3)
-        kx_x(0)
+        kx_z(1)
+        x_arrive(3)
+        kx_x(3)
         own_arrive(4)
-        kx_x(1)
-        own_arrive(5)
-        kx_z(0)
-        own_arrive(6)
-        kx_x(2)
-        kx_z(1)
-        own_arrive(0)
-        kx_x(3)
+        kx_z(2)
         x_arrive(0)
-        kx_z(2)
-        x_arrive(3)
-        own_arrive(1)
         x_arrive(4)
-        kx_z(3)
+        x_arrive(1)
         assemble(3)
         assemble(0)
+        kx_z(3)
+        own_arrive(5)
+        x_arrive(2)
+        assemble(4)
+        assemble(1)
         k_own.wait()
         k_part(tc).wait_recv()
 
@@ -385,29 +387,25 @@
 
         loop(0, KP, k_ready)
         d_load.wait()
-        x_arrive(1)
-        assemble(4)
-        assemble(1)
         forward(0)
         x_arrive(5)
+        assemble(2)
+        forward(1)
+        own_arrive(6)
+        loop(2, 4, forward)
+        x_arrive(6)
         assemble(5)
-        own_arrive(2)
         forward(4)
-        x_arrive(6)
         assemble(6)
-        x_arrive(2)
         loop(5, NH, forward)
-        assemble(2)
-        forward(3)
-        loop(1, 3, forward)
         zc = pltpu.make_async_copy(Dv, z_out, lM.at[0])
         zc.start()
 
-        def gw_chunk(q, co):
+        def gw_chunk(q, co, first=None):
             mine = NA if q < 2 else NB
 
             def part(k):
-                j = k if q < 2 else (k + 2) % 3
+                j = k if q < 2 else 2 - k
                 lhs = jnp.concatenate([AT[j, :, ROWS * i:ROWS * i + KROWS] for i in range(3)], axis=0)
                 r = jnp.dot(lhs, GP[co, 1:1 + HW].reshape(KROWS, CO), preferred_element_type=F32)
                 for i in range(3):
@@ -422,7 +420,18 @@
                     def _():
                         down(q, p).start()
 
-            loop(0, 3, part)
+            def part_step(k):
+                part(k)
+                if q == 2:
+
+                    @pl.when(k > 0)
+                    def _():
+                        step(first + k - 1)
+
+                if q == 3:
+                    step(first + k)
+
+            loop(0, 3, part_step)
 
         def chunk_of(q):
             return (t + 2 * (q // 2) + (1 - 2 * c) * (q % 2) + NG) % NG
@@ -464,24 +473,25 @@
             g_c(tx, v, 1).start()
 
         n = 0
-        for v, stop in zip((0, 4, 5, 6, 3, 1, 2), (0, 0, 1, 3, 5, 7, 8)):
+        for v, stop in enumerate((0, 0, 1, 3, 4, 6, 2 * NA)):
             relay(v)
             if stop > n:
                 loop(n, stop, step)
             n = stop
-        gw_chunk(2, tx)
+        gw_chunk(2, tx, n)
         loop(0, NH, lambda v: g_wait(txc, v))
-        gw_chunk(3, txc)
+        gw_chunk(3, txc, n + 2)
+        n = n + 5
         kb_own.wait()
         kb_part(1 - c).wait_recv()
         AC[...] = da_tap(0)
 
         def da_step(k):
-            step(n + k - 1)
-            AC[...] += da_tap(k)
-
-        loop(1, TAPS, da_step)
-        n = n + TAPS - 1
+            step(n + k)
+            AC[...] += da_tap(2 * k + 1) + da_tap(2 * k + 2)
+
+        loop(0, TAPS // 2, da_step)
+        n = n + TAPS // 2
         for g in range(NG):
             DA[g] = AC[...].reshape(NH, HW, NI, CO)[:, :, GI * g:GI * (g + 1), :].astype(BF)
             da_send(g).start()
@@ -508,7 +518,7 @@
             g_c(tx, u, 1).wait_send()
 
         loop(0, NH, drain_a)
-        loop(UX, NH, lambda u: a_x(u).wait_send())
+        loop(0, UX, lambda u: a_x(u).wait_send())
         L[0] = jnp.zeros(L.shape[1:], BF)
         zeros = pltpu.make_async_copy(L.at[0], da_out, lM.at[3])
         zeros.start()
@@ -550,14 +560,14 @@
         z_blk, da, gw = pl.pallas_call(
             body_kernel,
             out_shape=[
-                jax.ShapeDtypeStruct((HW, HW, NI, CO), BF),
-                jax.ShapeDtypeStruct((HW, HW, GI, CIN), BF),
-                jax.ShapeDtypeStruct((TAPS, CC, COUT), F32),
+                pltpu.VMEM((HW, HW, NI, CO), BF),
+                pltpu.VMEM((HW, HW, GI, CIN), BF),
+                pltpu.VMEM((TAPS, CC, COUT), F32),
             ],
             in_specs=[hbm, hbm, vmem, vmem, hbm],
-            out_specs=[hbm, hbm, hbm],
+            out_specs=[vmem, vmem, vmem],
             scratch_shapes=scratch,
-            compiler_params=pltpu.CompilerParams(collective_id=0, has_side_effects=True, vmem_limit_bytes=62 * 2**20),
+            compiler_params=pltpu.CompilerParams(collective_id=0, has_side_effects=True, vmem_limit_bytes=54 * 2**20),
             name="stage_conv",
         )(act, w_loc[0].reshape(TAPS, CC, COUT), scale_loc, shift_loc, dz)
         back = (2, 0, 1, 3)

time: 142 us -> 129 us (0.908)
  the two profiles are of different devices: /device:TPU:6 before, /device:TPU:19 now
where the time goes in v4:
time: 129 us
  Pallas kernels  124 us (96%)
  local copies, waits for them, and re-layouts  4.23 us (3%)
    pallas_call x1, Pallas kernels, body(): pl.pallas_call(body_kernel, out_shape=[pltpu.VMEM((HW, HW, NI, CO), BF),...  124 us
    unnamed x3, local copies, waits for them, and re-layouts  4.23 us

profile of v4, /device:TPU:19, one launch (start us, length us, event | category | flops | bytes accessed | tf_op | source)
XLA Modules:
  0.0 129.3 jit_solution(2507987287796441720)
XLA Ops:
  0.6 124.5 %stage_conv.1 = (bf16[14,14,16,256]{3,2,1,0:T(8,128)(2,1)S(1)}, bf16[14,14,4,512]{3,2,1,0:T(4,128)(2,1)S(1)}, f32[9,128,1024]{2,1,0:T(8,128)S(1)}) custom-call(bf16[14,14,4,512]{3,2,1,0:T(4,128)(2,1)} %bitcast.19, bf16[9,128,1024]{2,1,0:T(8,128)(2,1)} %bitcast.17, f32[1,256]{1,0:T(1,128)} %sc.1, f32[1,256]{1,0:T(1,128)} %sh.1, bf16[14,14,16,256]{3,2,1,0:T(8,128)(2,1)} %bitcast.18), custom_call_target="tpu_custom_call" | custom-call | tf_op jit(solution)/shard_map/stage_conv/pallas_call | solution.py:560
  125.1 1.2 copy.11
  126.3 0.9 copy.12
  127.1 2.2 %copy.13 = f32[1,3,3,128,1024]{4,3,2,1,0:T(8,128)} copy(f32[1,3,3,128,1024]{4,3,2,1,0:T(8,128)S(1)} %bitcast.14) | data formatting | bytes 9437184

commit v5 on v4

--- a/solution.py
+++ b/solution.py
@@ -18,10 +18,10 @@
 NG = 4
 GI = NI // NG
 TAPS = 9
-NA, NB = 5, 5
+NA, NB = 4, 6
 NROW = 2 * NA + 2 * NB
 NDET = NG * TAPS - NROW
-LMID, LEND, LEND0 = 3, 8, 6
+LMID, LEND, LEND0 = 3, 8, 5
 ROWS = PW * NI
 KROWS = HW * ROWS
 KH = 16
@@ -44,9 +44,9 @@
 
 def body_kernel(
     act, w, sc, sh, dz, z_out, da_out, gw_out,
-    IM, L, Kf, KX, Dv, AT, GP, PB, R1, R2, Kb, AC, DA, ZF,
+    IM, L, Kf, KX, Dv, AT, GP, PB, R1, R2, Kb, AC, DA,
     rA, sAy, sAx, sAc, rX, sXx, sXz, lK, sKc, rKc, lM, rG, sGx, sGc,
-    rP, sP, r1, r2, s1, s2, s3, so, sU, rD, sD,
+    rP, sP, r1, r2, s1, s2, s3, sU, rD, sD,
 ):
     z, y, t = lax.axis_index("dp"), lax.axis_index("stage"), lax.axis_index("tp")
     x, c = t // 2, t % 2
@@ -132,11 +132,11 @@
 
         @pl.when(z == 2)
         def _():
-            use(PB, q, p).start()
+            use(PB, q, p)
 
         @pl.when(z != 2)
         def _():
-            use(R2, q, p).start()
+            use(R2, q, p)
 
     def line_drain(q, p):
         @pl.when(z != 2)
@@ -183,21 +183,14 @@
             act_relay(u).start()
 
         loop(UX, NH, raise_rows)
-        ZF[...] = jnp.zeros(ZF.shape, F32)
-
-        def zfill(n):
-            return pltpu.make_async_copy(
-                ZF, gw_out.at[n // NG, :, lanes(CO * (n % NG), CO)], so.at[n % NG, n // NG])
-
-        loop(0, TAPS * NG, lambda n: zfill(n).start())
-
-        def zero_row(h):
-            Dv[h] = jnp.zeros(Dv.shape[1:], BF)
-
-        loop(0, HW, zero_row)
-        zc = pltpu.make_async_copy(Dv, z_out, lM.at[0])
-        zc.start()
-
+        def no_grad_w(tap):
+            gw_out[tap] = jnp.zeros((CC, COUT), F32)
+
+        def no_z(h):
+            z_out[h] = jnp.zeros((HW, NI, CO), BF)
+
+        loop(0, TAPS, no_grad_w)
+        loop(0, HW, no_z)
         lag0 = jnp.where(mid, LMID, LEND0)
 
         def step0(n):
@@ -211,7 +204,7 @@
             @pl.when((n >= lag0) & (n < NDET + lag0))
             def _():
                 q, p = detour_block(n - lag0)
-                line_final(q, p, up_final)
+                line_final(q, p, lambda src, q, p: up_final(src, q, p).start())
 
         loop(0, NDET + LEND0, step0)
 
@@ -221,11 +214,9 @@
             up_final(R2, q, p).wait_send()
 
         loop(0, NDET, drain)
-        loop(0, TAPS * NG, lambda n: zfill(n).wait())
         loop(0, NH, lambda u: act_up(u).wait_send())
         loop(UX, NH, lambda u: act_cross(t, u).wait_send())
         loop(UX, NH, lambda u: act_relay(u).wait_send())
-        zc.wait()
         loop(0, NG, lambda g: da_land(g).wait_recv())
 
     @pl.when(y == 1)
@@ -296,6 +287,11 @@
 
         loop(0, NG, gp_zero)
 
+        def no_grad_act(h):
+            da_out[h] = jnp.zeros((HW, GI, CIN), BF)
+
+        loop(0, HW, no_grad_act)
+
         def a_x(u):
             return copy_to(L.at[t, rows(u)], L.at[t, rows(u)], sAx.at[u], rA.at[t, u], dev_x)
 
@@ -351,7 +347,7 @@
             lin = pre.reshape(HC, HW, NI, CO) * scv + shv
             dv = Dv[rows(v)].astype(F32)
             GP[t, pl.ds(HC * v + 1, HC), 1:1 + HW] = jnp.where(lin > 0, dv * scv, 0.0).astype(BF)
-            Dv[rows(v)] = jnp.maximum(lin, 0.0).astype(BF)
+            z_out[rows(v)] = jnp.maximum(lin, 0.0).astype(BF)
             g_x(v).start()
             g_c(t, v, 0).start()
 
@@ -398,8 +394,6 @@
         forward(4)
         assemble(6)
         loop(5, NH, forward)
-        zc = pltpu.make_async_copy(Dv, z_out, lM.at[0])
-        zc.start()
 
         def gw_chunk(q, co, first=None):
             mine = NA if q < 2 else NB
@@ -436,9 +430,9 @@
         def chunk_of(q):
             return (t + 2 * (q // 2) + (1 - 2 * c) * (q % 2) + NG) % NG
 
-        def out_copy(src, q, p):
+        def put(src, q, p):
             tap = 3 * (p % 3) + p // 3
-            return pltpu.make_async_copy(src.at[q, p], gw_out.at[tap, :, lanes(CO * chunk_of(q), CO)], so.at[q, p])
+            gw_out[tap, :, lanes(CO * chunk_of(q), CO)] = src[q, p]
 
         def step(n):
             @pl.when(n < NROW)
@@ -448,7 +442,7 @@
             @pl.when((n >= lag) & (n < NROW + lag))
             def _():
                 q, p = row_block(n - lag)
-                line_final(q, p, out_copy)
+                line_final(q, p, put)
 
         def da_tap(tap):
             i, j = tap // 3, tap % 3
@@ -500,7 +494,7 @@
         def detour(m):
             q, p = detour_block(m)
             up_final(R2, q, p).wait_recv()
-            out_copy(R2, q, p).start()
+            put(R2, q, p)
 
         loop(0, NDET, detour)
 
@@ -519,15 +513,9 @@
 
         loop(0, NH, drain_a)
         loop(0, UX, lambda u: a_x(u).wait_send())
-        L[0] = jnp.zeros(L.shape[1:], BF)
-        zeros = pltpu.make_async_copy(L.at[0], da_out, lM.at[3])
-        zeros.start()
         loop(0, NROW, lambda m: line_drain(*row_block(m)))
         loop(0, NDET, lambda m: down(*detour_block(m)).wait_send())
-        loop(0, TAPS * NG, lambda m: out_copy(R2, m // TAPS, m % TAPS).wait())
         loop(0, NG, lambda g: da_send(g).wait_send())
-        zc.wait()
-        zeros.wait()
 
 
 def solution(mesh):
@@ -550,11 +538,10 @@
             pltpu.VMEM((TAPS, 2 * CC, COUT), BF),
             pltpu.VMEM((NH * HW * NI, CO), F32),
             pltpu.VMEM((NG, NH, HW, GI, CO), BF),
-            pltpu.VMEM((CC, CO), F32),
             dma((NG, NH)), dma((NH,)), dma((NH,)), dma((2, NH)),
             dma((KP,)), dma((KHALF,)), dma((KHALF,)), dma((KP + 1,)), dma((KP + 2,)), dma((KP + 2,)), dma((4,)),
             dma((NG, NH)), dma((NH,)), dma((2, NH)),
-        ] + [dma(block)] * 9 + [dma((NG,)), dma((NG,))]
+        ] + [dma(block)] * 8 + [dma((NG,)), dma((NG,))]
         act = jnp.transpose(act_loc[0], (1, 2, 0, 3))
         dz = jnp.transpose(grad_loc[0], (1, 2, 0, 3))
         z_blk, da, gw = pl.pallas_call(

time: 129 us -> 128 us (level)
  the two profiles are of different devices: /device:TPU:19 before, /device:TPU:0 now
where the time goes in v5:
time: 128 us; the launch traced here: 127 us
  Pallas kernels  123 us (96%)
  local copies, waits for them, and re-layouts  4.23 us (3%)
    pallas_call x1, Pallas kernels, body(): pl.pallas_call(body_kernel, out_shape=[pltpu.VMEM((HW, HW, NI, CO), BF),...  123 us
    unnamed x3, local copies, waits for them, and re-layouts  4.23 us

profile of v5, /device:TPU:0, one launch (start us, length us, event | category | flops | bytes accessed | tf_op | source)
XLA Modules:
  0.0 127.5 jit_solution(15521033216372859327)
XLA Ops:
  0.6 122.6 %stage_conv.1 = (bf16[14,14,16,256]{3,2,1,0:T(8,128)(2,1)S(1)}, bf16[14,14,4,512]{3,2,1,0:T(4,128)(2,1)S(1)}, f32[9,128,1024]{2,1,0:T(8,128)S(1)}) custom-call(bf16[14,14,4,512]{3,2,1,0:T(4,128)(2,1)} %bitcast.19, bf16[9,128,1024]{2,1,0:T(8,128)(2,1)} %bitcast.17, f32[1,256]{1,0:T(1,128)} %sc.1, f32[1,256]{1,0:T(1,128)} %sh.1, bf16[14,14,16,256]{3,2,1,0:T(8,128)(2,1)} %bitcast.18), custom_call_target="tpu_custom_call" | custom-call | tf_op jit(solution)/shard_map/stage_conv/pallas_call | solution.py:547
  123.2 1.2 copy.11
  124.4 0.9 copy.12
  125.3 2.2 %copy.13 = f32[1,3,3,128,1024]{4,3,2,1,0:T(8,128)} copy(f32[1,3,3,128,1024]{4,3,2,1,0:T(8,128)S(1)} %bitcast.14) | data formatting | bytes 9437184
